TPU v7x, 32 devices: a whole 2x2x4 slice. The times are simulated.
32 devices in a mesh: dp: 4 (over z), expert: 2 (over x), shard: 4 (over y, core).
Axes of the slice: x: 2, y: 2, z: 4, core: 2. Of those that a mesh axis runs over, the one named last changes fastest.
Arguments:
- activations: bfloat16 [2, 2, 2048, 256], P(None, 'expert', ('dp', 'shard')), may hold values from -6 to 6
- out_grads: bfloat16 [2, 2, 2048, 14336], P(None, 'expert', ('dp', 'shard')), may hold values from -0.25 to 0.25
- weights: float32 [2, 2, 256, 14336], P(None, 'expert', ('dp', 'shard')), may hold values from -4 to 4
- shadow: float32 [2, 2, 256, 14336], P(None, 'expert', ('dp', 'shard')), may hold values from -4 to 4
- counts: int32 [2, 32, 2], P(None, ('dp', 'expert', 'shard')), may hold values from 1 to 1024, as said below
Outputs:
- new_weights: float32 [2, 2, 256, 14336], P(None, 'expert', ('dp', 'shard'))
- new_shadow: float32 [2, 2, 256, 14336], P(None, 'expert', ('dp', 'shard'))
Inputs may be any that keep to these rules, and one draw needn't show every extreme that they name: `counts`: loads differ between the experts of a layer.
All inputs are finite; a program needn't handle non-finite values.
Results may differ from a plain program's by a relative error of at most 0.0003.
Values sent between devices are 32-bit elements; how exact they have to be, the bound alone decides.
A program may use at most 128 MiB of HBM per device.

v0:
```python
import functools

import jax
import jax.numpy as jnp
from jax import lax
from jax.experimental import pallas as pl
from jax.experimental.pallas import tpu as pltpu
from jax.sharding import PartitionSpec as P

step_size = 0.5
clip_level = 1.0
CORES = 2
SLOTS = 4
LAG = 3
COLS = 256
MESH = pl.DeviceIdType.MESH


def kernel(
    dims, rows_ref, cot_ref, cnt_ref, out_ref, stat_ref,
    merged, from_y, from_z, from_zx, late_y, staged, squares, seen, message, gathered,
    core_send, core_recv, y_send, y_recv, z_send, z_recv, zx_send, zx_recv,
    late_send, late_recv, cnt_send, cnt_recv, all_send, all_recv,
):
    line, experts, shards, layers, per_layer, width, rows, numel = dims
    group = line * shards
    half = line * rows
    chunks = layers * per_layer
    z, e, s = lax.axis_index("dp"), lax.axis_index("expert"), lax.axis_index("shard")
    y, c = s // CORES, s % CORES
    me = z * shards + s
    core_peer = {"shard": y * CORES + (1 - c)}
    y_peer = {"shard": (1 - y) * CORES + c}
    own, other = y * half, (1 - y) * half

    def group_peer(d):
        p = lax.rem(me + d, group)
        return p, {"dp": p // shards, "shard": p % shards}

    def remote(src, dst, send, recv, device):
        return pltpu.make_async_remote_copy(
            src_ref=src, dst_ref=dst, send_sem=send, recv_sem=recv,
            device_id=device, device_id_type=MESH,
        )

    barrier = pltpu.get_barrier_semaphore()
    for d in range(1, group):
        pl.semaphore_signal(barrier, inc=1, device_id=group_peer(d)[1], device_id_type=MESH)
    for d in range(1, experts):
        pl.semaphore_signal(
            barrier, inc=1, device_id={"expert": lax.rem(e + d, experts)}, device_id_type=MESH
        )
    pl.semaphore_wait(barrier, group + experts - 2)

    def count_copy(d, sender):
        return remote(
            cnt_ref, seen.at[sender], cnt_send.at[d], cnt_recv.at[sender],
            {"expert": lax.rem(e + d, experts)},
        )

    for d in range(1, experts):
        count_copy(d, e).start()
    squares[...] = jnp.zeros_like(squares)

    def place(k):
        return k // per_layer, k % per_layer

    def when_chunk(k, body):
        pl.when((k >= 0) & (k < chunks))(lambda: body(k))

    def core_copy(k):
        return remote(
            staged.at[k % SLOTS], merged.at[k], core_send.at[k % SLOTS], core_recv.at[k], core_peer
        )

    def y_copy(k):
        return remote(
            merged.at[k, pl.ds(pl.multiple_of(other, 8), half)], from_y.at[k],
            y_send.at[k], y_recv.at[k], y_peer,
        )

    def late_copy(layer):
        k = layer * per_layer
        return remote(
            merged.at[k, pl.ds(pl.multiple_of(other + z * rows, 8), rows)], late_y.at[layer],
            late_send.at[layer], late_recv.at[layer], y_peer,
        )

    def product(layer, q, core, i):
        at = pl.ds(pl.multiple_of(q * width + i * COLS, 128), COLS)
        return jnp.dot(
            rows_ref[layer, core], cot_ref[layer, :, at], preferred_element_type=jnp.float32
        )

    def stage_partner(k):
        layer, q = place(k)
        pl.when(k >= SLOTS)(lambda: core_copy(k - SLOTS).wait_send())

        def tile(i, _):
            at = pl.ds(pl.multiple_of(i * COLS, 128), COLS)
            staged[k % SLOTS, :, at] = product(layer, q, 1 - c, i)
            return 0

        lax.fori_loop(0, width // COLS, tile, 0)
        core_copy(k).start()

    def merge_core(k):
        layer, q = place(k)
        core_copy(k).wait_recv()

        def tile(i, _):
            at = pl.ds(pl.multiple_of(i * COLS, 128), COLS)
            merged[k, :, at] = merged[k, :, at] + product(layer, q, c, i)
            return 0

        lax.fori_loop(0, width // COLS, tile, 0)
        pl.when(q > 0)(lambda: y_copy(k).start())

    def merge_y(k):
        @pl.when(k % per_layer > 0)
        def _():
            y_copy(k).wait_recv()
            at = pl.ds(pl.multiple_of(own, 8), half)
            merged[k, at, :] = merged[k, at, :] + from_y[k]

    def block(k, base, b):
        return merged.at[k, pl.ds(pl.multiple_of(base + b * rows, 8), rows)]

    def z_copy(k, base, b, slot, device, extra):
        layer = k // per_layer
        if extra:
            return remote(
                block(k, base, b), from_zx.at[layer, slot], zx_send.at[layer, b],
                zx_recv.at[layer, slot], device,
            )
        return remote(
            block(k, base, b), from_z.at[k, slot], z_send.at[k, b], z_recv.at[k, slot], device
        )

    def arrived(k, slot, extra):
        return from_zx[k // per_layer, slot] if extra else from_z[k, slot]

    def add_arrived(k, base, b, slot, extra):
        z_copy(k, base, b, slot, {"dp": z}, extra).wait_recv()
        ref = block(k, base, b)
        ref[...] = ref[...] + arrived(k, slot, extra)

    def to_right(k, base, extra):
        for b in reversed(range(1, line)):
            @pl.when(z < b)
            def _():
                pl.when(z > 0)(lambda: add_arrived(k, base, b, b + 1, extra))
                z_copy(k, base, b, b + 1, {"dp": z + 1}, extra).start()

    def to_left(k, base, extra):
        for b in range(line - 1):
            @pl.when(z > b)
            def _():
                pl.when(z < line - 1)(lambda: add_arrived(k, base, b, b, extra))
                z_copy(k, base, b, b, {"dp": z - 1}, extra).start()

    def both_halves(pass_one):
        def body(k):
            pl.when(k % per_layer == 0)(lambda: pass_one(k, other, True))
            pass_one(k, own, False)
        return body

    def put(k, values):
        layer, q = place(k)
        out_ref[layer, :, pl.ds(pl.multiple_of(q * width, 128), width)] = values
        squares[layer] = squares[layer] + values * values

    def finish_one(k, base, extra):
        pl.when(z > 0)(lambda: add_arrived(k, base, z, z + 1, extra))
        pl.when(z < line - 1)(lambda: add_arrived(k, base, z, z, extra))
        if extra:
            late_copy(k // per_layer).start()
        else:
            pl.when(k % per_layer > 0)(lambda: put(k, block(k, base, z)[...]))

    def step(t, _):
        when_chunk(t, stage_partner)
        when_chunk(t - 1, merge_core)
        when_chunk(t - LAG, merge_y)
        back = line - 1 - z
        when_chunk(t - LAG - z, both_halves(to_right))
        when_chunk(t - LAG - back, both_halves(to_left))
        when_chunk(t - LAG - jnp.maximum(z, back), both_halves(finish_one))
        return 0

    lax.fori_loop(0, chunks + LAG + line - 1, step, 0)

    for layer in range(layers):
        late_copy(layer).wait_recv()
        put(layer * per_layer, block(layer * per_layer, own, z)[...] + late_y[layer])

    totals = cnt_ref[...]
    for d in range(1, experts):
        sender = lax.rem(e + d, experts)
        count_copy(d, sender).wait_recv()
        totals = totals + seen[sender]
    row = lax.broadcasted_iota(jnp.int32, totals.shape, 0)
    lane = lax.broadcasted_iota(jnp.int32, totals.shape, 1)
    for layer in range(layers):
        share = jnp.sum(jnp.sum(squares[layer], axis=0, keepdims=True), axis=1, keepdims=True)
        totals = jnp.where(row == layer, share, totals)
    message[...] = totals
    gathered[me] = totals

    def all_copy(d, sender):
        return remote(
            message, gathered.at[sender], all_send.at[d], all_recv.at[sender], group_peer(d)[1]
        )

    for d in range(1, group):
        all_copy(d, me).start()
    for d in range(1, group):
        all_copy(d, group_peer(d)[0]).wait_recv()
    total = gathered[0]
    for p in range(1, group):
        total = total + gathered[p]
    stats = jnp.zeros_like(total)
    for layer in range(layers):
        loads = total[layers + layer:layers + layer + 1, :]
        spot = lane[:1]
        own_load = jnp.sum(jnp.where(spot == e, loads, 0.0), axis=1, keepdims=True)
        mean_load = jnp.sum(jnp.where(spot < experts, loads, 0.0), axis=1, keepdims=True) / experts
        root_mean = jnp.sqrt(total[layer:layer + 1, :1] / numel)
        factor = (
            step_size * (own_load / mean_load) * clip_level / jnp.maximum(root_mean, clip_level)
        )
        beta = own_load / (own_load + mean_load)
        stats = jnp.where(row == layer, factor, stats)
        stats = jnp.where(row == layers + layer, beta, stats)
    stat_ref[...] = stats

    for d in range(1, group):
        all_copy(d, me).wait_send()
    for d in range(1, experts):
        count_copy(d, e).wait_send()
    for k in range(chunks - min(SLOTS, chunks), chunks):
        core_copy(k).wait_send()

    def drain(k, _):
        pl.when(k % per_layer > 0)(lambda: y_copy(k).wait_send())
        for b in range(line):
            pl.when(z != b)(lambda: z_copy(k, own, b, b, {"dp": z}, False).wait_send())
        return 0

    lax.fori_loop(0, chunks, drain, 0)
    for layer in range(layers):
        late_copy(layer).wait_send()
        for b in range(line):
            pl.when(z != b)(
                lambda: z_copy(layer * per_layer, other, b, b, {"dp": z}, True).wait_send()
            )


def on_device(sizes, activations, out_grads, weights, shadow, counts):
    line, experts, shards = sizes
    layers, _, tokens, all_rows = activations.shape
    ff, rows = out_grads.shape[3], weights.shape[2]
    assert shards == 2 * CORES and 2 * layers <= 8
    units = ff // 128
    per_layer = next(p for p in range(6, units + 1) if units % p == 0 and units // p % 2 == 0)
    width = ff // per_layer
    chunks = layers * per_layer
    half = line * rows
    group = line * shards
    acts = activations[:, 0].reshape(layers, tokens, line, shards // CORES, CORES, rows)
    acts = acts.transpose(0, 4, 3, 2, 5, 1).reshape(layers, CORES, all_rows // CORES, tokens)
    tile = jnp.pad(
        counts[:, 0, :].astype(jnp.float32), ((layers, 8 - 2 * layers), (0, 128 - experts))
    )
    f32 = jnp.float32
    dma = pltpu.SemaphoreType.DMA
    vmem = pl.BlockSpec(memory_space=pltpu.VMEM)
    dims = (line, experts, shards, layers, per_layer, width, rows, all_rows * ff)
    summed, stats = pl.pallas_call(
        functools.partial(kernel, dims),
        out_shape=(
            jax.ShapeDtypeStruct((layers, rows, ff), f32), jax.ShapeDtypeStruct((8, 128), f32)
        ),
        in_specs=[vmem] * 3,
        out_specs=(vmem, vmem),
        scratch_shapes=[
            pltpu.VMEM((chunks, 2 * half, width), f32),
            pltpu.VMEM((chunks, half, width), f32),
            pltpu.VMEM((chunks, line + 1, rows, width), f32),
            pltpu.VMEM((layers, line + 1, rows, width), f32),
            pltpu.VMEM((layers, rows, width), f32),
            pltpu.VMEM((SLOTS, 2 * half, width), f32),
            pltpu.VMEM((layers, rows, width), f32),
            pltpu.VMEM((experts, 8, 128), f32),
            pltpu.VMEM((8, 128), f32),
            pltpu.VMEM((group, 8, 128), f32),
            dma((SLOTS,)), dma((chunks,)), dma((chunks,)), dma((chunks,)),
            dma((chunks, line)), dma((chunks, line + 1)),
            dma((layers, line)), dma((layers, line + 1)),
            dma((layers,)), dma((layers,)), dma((experts,)), dma((experts,)),
            dma((group,)), dma((group,)),
        ],
        compiler_params=pltpu.CompilerParams(
            collective_id=0, has_side_effects=True, vmem_limit_bytes=62 * 1024 * 1024
        ),
        name="reduce_gradient",
    )(acts, out_grads[:, 0], tile)
    factor = stats[:layers, 0][:, None, None]
    beta = stats[layers:2 * layers, 0][:, None, None]
    updated = weights[:, 0] - factor * summed
    previous = shadow[:, 0]
    return updated[:, None], (previous + beta * (updated - previous))[:, None]


def solution(mesh):
    rows = P(None, "expert", ("dp", "shard"), None)
    in_specs = (rows, rows, rows, rows, P(None, ("dp", "expert", "shard"), None))
    sizes = tuple(mesh.shape[a] for a in ("dp", "expert", "shard"))
    return jax.shard_map(
        functools.partial(on_device, sizes), mesh=mesh, in_specs=in_specs,
        out_specs=(rows, rows), check_vma=False,
    )
```

profile of v0, /device:TPU:0, one launch (start us, length us, event | category | flops | bytes accessed | tf_op | source)
XLA Modules:
  0.0 191.1 jit_solution(6211625333718271075)
XLA Ops:
  0.6 0.7 convert_element_type.8
  1.3 0.6 pad.4.cnt_ref
  1.9 1.0 copy.10
  2.9 0.7 copy.11
  3.6 0.0 copy-start
  3.6 182.3 %reduce_gradient.1 = (f32[2,16,14336]{2,1,0:T(8,128)}, f32[8,128]{1,0:T(8,128)}) custom-call(bf16[2,2,128,128]{3,2,1,0:T(8,128)(2,1)} %bitcast.30, bf16[2,128,14336]{2,1,0:T(8,128)(2,1)} %bitcast.29, f32[8,128]{1,0:T(8,128)} %pad.4.cnt_ref), custom_call_target="tpu_custom_call" | custom-call | tf_op jit(solution)/shard_map/reduce_gradient/pallas_call | solution.py:279
  185.9 0.9 slice_reduce_fusion
  186.8 0.0 copy-done
  186.8 4.3 %fusion.1 = (f32[2,1,16,14336]{3,2,1,0:T(8,128)}, f32[2,1,16,14336]{3,2,1,0:T(8,128)}) fusion(f32[2,1,16,14336]{3,2,1,0:T(8,128)S(1)} %copy-done, f32[2]{0:T(128)S(1)} %get-tuple-element.10, f32[2,16,14336]{2,1,0:T(8,128)} %get-tuple-element.5, f32[2]{0:T(128)S(1)} %get-tuple-element.11, f32[2,1,16,14336]{3,2,1,0:T(8,128)} %param.7), kind=kLoop, calls=%fused_computation.3 | loop fusion | flops 2293760 | bytes 9175056
Async XLA Ops:
  3.6 183.2 %copy-start = (f32[2,1,16,14336]{3,2,1,0:T(8,128)S(1)}, f32[2,1,16,14336]{3,2,1,0:T(8,128)}, u32[]{:S(2)}) copy-start(f32[2,1,16,14336]{3,2,1,0:T(8,128)} %param.8) | copy-start | bytes 5505028
where the time goes:
time: 191 us
  Pallas kernels  182 us (95%)
  other arithmetic  4.98 us (3%)
  local copies, waits for them, and re-layouts  3.2 us (2%)
    pallas_call x1, Pallas kernels, on_device(): pl.pallas_call(functools.partial(kernel, dims), out_shape=(jax.ShapeDtype...  182 us
    unnamed x1, other arithmetic  4.29 us

commit v1 on v0

v1 whole, which is shorter than its diff:
```python
import functools

import jax
import jax.numpy as jnp
from jax import lax
from jax.experimental import pallas as pl
from jax.experimental.pallas import tpu as pltpu
from jax.sharding import PartitionSpec as P

step_size = 0.5
clip_level = 1.0
CORES = 2
SLOTS = 4
LAG = 5
HOP = 2
HOP_LATE = 4
AHEAD = 6
RING = 8
PIECES = 28
MESH = pl.DeviceIdType.MESH


def kernel(
    dims, acts, cot_hbm, cnt, out_ref, stat_ref,
    turned, rows_ref, cot, merged, from_y, from_z, from_zx, late_y, staged,
    squares, counted, seen, message, gathered,
    cot_sem, core_send, core_recv, y_send, y_recv, z_send, z_recv,
    zx_send, zx_recv, late_send, late_recv, cnt_send, cnt_recv, all_send, all_recv,
):
    line, experts, shards, layers, per_layer, width, rows, numel, period, lates = dims
    group = line * shards
    half = line * rows
    chunks = layers * per_layer
    z, e, s = lax.axis_index("dp"), lax.axis_index("expert"), lax.axis_index("shard")
    y, c = s // CORES, s % CORES
    me = z * shards + s
    core_peer = {"shard": y * CORES + (1 - c)}
    y_peer = {"shard": (1 - y) * CORES + c}
    own, other = y * half, (1 - y) * half

    def place(k):
        return k // per_layer, k % per_layer

    def columns(q):
        return pl.ds(pl.multiple_of(q * width, 128), width)

    def fetch(k):
        layer, q = place(k)
        return pltpu.make_async_copy(
            cot_hbm.at[layer, :, columns(q)], cot.at[k % RING], cot_sem.at[k % RING]
        )

    for k in range(min(AHEAD, chunks)):
        fetch(k).start()

    def group_peer(d):
        p = lax.rem(me + d, group)
        return p, {"dp": p // shards, "shard": p % shards}

    def remote(src, dst, send, recv, device):
        return pltpu.make_async_remote_copy(
            src_ref=src, dst_ref=dst, send_sem=send, recv_sem=recv,
            device_id=device, device_id_type=MESH,
        )

    barrier = pltpu.get_barrier_semaphore()
    for d in range(1, group):
        pl.semaphore_signal(barrier, inc=1, device_id=group_peer(d)[1], device_id_type=MESH)
    for d in range(1, experts):
        pl.semaphore_signal(
            barrier, inc=1, device_id={"expert": lax.rem(e + d, experts)}, device_id_type=MESH
        )

    for layer in range(layers):
        across = acts[layer].astype(jnp.float32).T
        for b in range(line):
            for h in range(shards // CORES):
                for core in range(CORES):
                    at = ((b * (shards // CORES) + h) * CORES + core) * rows
                    to = (h * line + b) * rows
                    turned[core, to:to + rows, :] = across[at:at + rows]
        for core in range(CORES):
            rows_ref[layer, core] = turned[core].astype(rows_ref.dtype)

    row = lax.broadcasted_iota(jnp.int32, counted.shape, 0)
    lane = lax.broadcasted_iota(jnp.int32, counted.shape, 1)
    tile = jnp.zeros(counted.shape, jnp.float32)
    for layer in range(layers):
        for p in range(experts):
            here = (row == layers + layer) & (lane == p)
            tile = jnp.where(here, cnt[layer, 0, p].astype(jnp.float32), tile)
    counted[...] = tile
    squares[...] = jnp.zeros_like(squares)

    pl.semaphore_wait(barrier, group + experts - 2)

    def count_copy(d, sender):
        return remote(
            counted, seen.at[sender], cnt_send.at[d], cnt_recv.at[sender],
            {"expert": lax.rem(e + d, experts)},
        )

    for d in range(1, experts):
        count_copy(d, e).start()

    def is_late(k):
        return (k % period == 1) & (k < period * lates)

    def when_chunk(k, body):
        pl.when((k >= 0) & (k < chunks))(lambda: body(k))

    def when_early(k, body):
        when_chunk(k, lambda k: pl.when(jnp.logical_not(is_late(k)))(lambda: body(k)))

    def when_late(k, body):
        when_chunk(k, lambda k: pl.when(is_late(k))(lambda: body(k)))

    def core_copy(k):
        return remote(
            staged.at[k % SLOTS], merged.at[k], core_send.at[k % SLOTS], core_recv.at[k], core_peer
        )

    def y_copy(k):
        return remote(
            merged.at[k, pl.ds(pl.multiple_of(other, 8), half)], from_y.at[k],
            y_send.at[k], y_recv.at[k], y_peer,
        )

    def late_copy(k):
        j = k // period
        return remote(
            merged.at[k, pl.ds(pl.multiple_of(other + z * rows, 8), rows)], late_y.at[j],
            late_send.at[j], late_recv.at[j], y_peer,
        )

    def product(k, core):
        layer, _ = place(k)
        return jnp.dot(
            rows_ref[layer, core], cot[k % RING], preferred_element_type=jnp.float32
        )

    def stage_partner(k):
        pl.when(k >= SLOTS)(lambda: core_copy(k - SLOTS).wait_send())
        fetch(k).wait()
        staged[k % SLOTS] = product(k, 1 - c)
        core_copy(k).start()

    def merge_core(k):
        core_copy(k).wait_recv()
        merged[k] = merged[k] + product(k, c)
        pl.when(jnp.logical_not(is_late(k)))(lambda: y_copy(k).start())

    def merge_y(k):
        y_copy(k).wait_recv()
        at = pl.ds(pl.multiple_of(own, 8), half)
        merged[k, at, :] = merged[k, at, :] + from_y[k]

    def block(k, base, b):
        return merged.at[k, pl.ds(pl.multiple_of(base + b * rows, 8), rows)]

    def z_copy(k, base, b, slot, device, extra):
        if extra:
            j = k // period
            return remote(
                block(k, base, b), from_zx.at[j, slot], zx_send.at[j, b], zx_recv.at[j, slot],
                device,
            )
        return remote(
            block(k, base, b), from_z.at[k, slot], z_send.at[k, b], z_recv.at[k, slot], device
        )

    def arrived(k, slot, extra):
        return from_zx[k // period, slot] if extra else from_z[k, slot]

    def add_arrived(k, base, b, slot, extra):
        z_copy(k, base, b, slot, {"dp": z}, extra).wait_recv()
        ref = block(k, base, b)
        ref[...] = ref[...] + arrived(k, slot, extra)

    def to_right(k, base, extra):
        for b in reversed(range(1, line)):
            @pl.when(z < b)
            def _():
                pl.when(z > 0)(lambda: add_arrived(k, base, b, b + 1, extra))
                z_copy(k, base, b, b + 1, {"dp": z + 1}, extra).start()

    def to_left(k, base, extra):
        for b in range(line - 1):
            @pl.when(z > b)
            def _():
                pl.when(z < line - 1)(lambda: add_arrived(k, base, b, b, extra))
                z_copy(k, base, b, b, {"dp": z - 1}, extra).start()

    def both_halves(one):
        def body(k):
            one(k, other, True)
            one(k, own, False)
        return body

    def own_half(one):
        return lambda k: one(k, own, False)

    def put(k, values):
        layer, q = place(k)
        out_ref[layer, :, columns(q)] = values
        squares[layer] = squares[layer] + values * values

    def gather_block(k, base, extra):
        pl.when(z > 0)(lambda: add_arrived(k, base, z, z + 1, extra))
        pl.when(z < line - 1)(lambda: add_arrived(k, base, z, z, extra))

    def finish_early(k):
        gather_block(k, own, False)
        put(k, block(k, own, z)[...])

    def finish_late(k):
        gather_block(k, other, True)
        late_copy(k).start()
        gather_block(k, own, False)

    back = line - 1 - z
    far = jnp.maximum(z, back)

    def step(t, _):
        pl.when(t + AHEAD < chunks)(lambda: fetch(t + AHEAD).start())
        when_chunk(t, stage_partner)
        when_chunk(t - 1, merge_core)
        when_late(t - 1 - HOP_LATE * z, both_halves(to_right))
        when_late(t - 1 - HOP_LATE * back, both_halves(to_left))
        when_late(t - 1 - HOP_LATE * far, finish_late)
        when_early(t - LAG, merge_y)
        when_early(t - LAG - HOP * z, own_half(to_right))
        when_early(t - LAG - HOP * back, own_half(to_left))
        when_early(t - LAG - HOP * far, finish_early)
        return 0

    steps = chunks + LAG + HOP * (line - 1)
    steps = max(steps, period * (lates - 1) + 3 + HOP_LATE * (line - 1))
    lax.fori_loop(0, steps, step, 0)

    def add_late(j, _):
        k = j * period + 1
        late_copy(k).wait_recv()
        put(k, block(k, own, z)[...] + late_y[j])
        return 0

    lax.fori_loop(0, lates, add_late, 0)

    totals = counted[...]
    for d in range(1, experts):
        sender = lax.rem(e + d, experts)
        count_copy(d, sender).wait_recv()
        totals = totals + seen[sender]
    for layer in range(layers):
        share = jnp.sum(jnp.sum(squares[layer], axis=0, keepdims=True), axis=1, keepdims=True)
        totals = jnp.where(row == layer, share, totals)
    message[...] = totals
    gathered[me] = totals

    def all_copy(d, sender):
        return remote(
            message, gathered.at[sender], all_send.at[d], all_recv.at[sender], group_peer(d)[1]
        )

    for d in range(1, group):
        all_copy(d, me).start()
    for d in range(1, group):
        all_copy(d, group_peer(d)[0]).wait_recv()
    total = gathered[0]
    for p in range(1, group):
        total = total + gathered[p]
    stats = jnp.zeros_like(total)
    for layer in range(layers):
        loads = total[layers + layer:layers + layer + 1, :]
        spot = lane[:1]
        own_load = jnp.sum(jnp.where(spot == e, loads, 0.0), axis=1, keepdims=True)
        mean_load = jnp.sum(jnp.where(spot < experts, loads, 0.0), axis=1, keepdims=True) / experts
        root_mean = jnp.sqrt(total[layer:layer + 1, :1] / numel)
        factor = (
            step_size * (own_load / mean_load) * clip_level / jnp.maximum(root_mean, clip_level)
        )
        beta = own_load / (own_load + mean_load)
        stats = jnp.where(row == layer, factor, stats)
        stats = jnp.where(row == layers + layer, beta, stats)
    stat_ref[...] = stats

    for d in range(1, group):
        all_copy(d, me).wait_send()
    for d in range(1, experts):
        count_copy(d, e).wait_send()
    for k in range(chunks - min(SLOTS, chunks), chunks):
        core_copy(k).wait_send()

    def drain(k, _):
        pl.when(jnp.logical_not(is_late(k)))(lambda: y_copy(k).wait_send())
        for b in range(line):
            pl.when(z != b)(lambda: z_copy(k, own, b, b, {"dp": z}, False).wait_send())
        return 0

    def drain_late(j, _):
        k = j * period + 1
        late_copy(k).wait_send()
        for b in range(line):
            pl.when(z != b)(lambda: z_copy(k, other, b, b, {"dp": z}, True).wait_send())
        return 0

    lax.fori_loop(0, chunks, drain, 0)
    lax.fori_loop(0, lates, drain_late, 0)


def on_device(sizes, activations, out_grads, weights, shadow, counts):
    line, experts, shards = sizes
    layers, _, tokens, all_rows = activations.shape
    ff, rows = out_grads.shape[3], weights.shape[2]
    assert shards == 2 * CORES and 2 * layers <= 8
    units = ff // 128
    per_layer = next(
        p for p in range(PIECES, units + 1) if units % p == 0 and units // p % 2 == 0
    )
    width = ff // per_layer
    chunks = layers * per_layer
    half = line * rows
    group = line * shards
    period = max(2, 2 * (line - 1))
    lates = chunks // period
    f32 = jnp.float32
    dma = pltpu.SemaphoreType.DMA
    vmem = pl.BlockSpec(memory_space=pltpu.VMEM)
    hbm = pl.BlockSpec(memory_space=pltpu.HBM)
    dims = (line, experts, shards, layers, per_layer, width, rows, all_rows * ff, period, lates)
    summed, stats = pl.pallas_call(
        functools.partial(kernel, dims),
        out_shape=(
            jax.ShapeDtypeStruct((layers, rows, ff), f32), jax.ShapeDtypeStruct((8, 128), f32)
        ),
        in_specs=[vmem, hbm, pl.BlockSpec(memory_space=pltpu.SMEM)],
        out_specs=(vmem, vmem),
        scratch_shapes=[
            pltpu.VMEM((CORES, 2 * half, tokens), f32),
            pltpu.VMEM((layers, CORES, 2 * half, tokens), activations.dtype),
            pltpu.VMEM((RING, tokens, width), out_grads.dtype),
            pltpu.VMEM((chunks, 2 * half, width), f32),
            pltpu.VMEM((chunks, half, width), f32),
            pltpu.VMEM((chunks, line + 1, rows, width), f32),
            pltpu.VMEM((lates, line + 1, rows, width), f32),
            pltpu.VMEM((lates, rows, width), f32),
            pltpu.VMEM((SLOTS, 2 * half, width), f32),
            pltpu.VMEM((layers, rows, width), f32),
            pltpu.VMEM((8, 128), f32),
            pltpu.VMEM((experts, 8, 128), f32),
            pltpu.VMEM((8, 128), f32),
            pltpu.VMEM((group, 8, 128), f32),
            dma((RING,)),
            dma((SLOTS,)), dma((chunks,)), dma((chunks,)), dma((chunks,)),
            dma((chunks, line)), dma((chunks, line + 1)),
            dma((lates, line)), dma((lates, line + 1)),
            dma((lates,)), dma((lates,)), dma((experts,)), dma((experts,)),
            dma((group,)), dma((group,)),
        ],
        compiler_params=pltpu.CompilerParams(
            collective_id=0, has_side_effects=True, vmem_limit_bytes=46 * 1024 * 1024
        ),
        name="reduce_gradient",
    )(activations[:, 0], out_grads[:, 0], counts)
    factor = stats[:layers, 0][:, None, None]
    beta = stats[layers:2 * layers, 0][:, None, None]
    updated = weights[:, 0] - factor * summed
    previous = shadow[:, 0]
    return updated[:, None], (previous + beta * (updated - previous))[:, None]


def solution(mesh):
    rows = P(None, "expert", ("dp", "shard"), None)
    in_specs = (rows, rows, rows, rows, P(None, ("dp", "expert", "shard"), None))
    sizes = tuple(mesh.shape[a] for a in ("dp", "expert", "shard"))
    return jax.shard_map(
        functools.partial(on_device, sizes), mesh=mesh, in_specs=in_specs,
        out_specs=(rows, rows), check_vma=False,
    )
```

time: 191 us -> 175 us (0.916)
  Pallas kernels: 182 us -> 170 us
  other arithmetic: 4.98 us -> 2.41 us
    pallas_call x1, Pallas kernels: 182 us -> 170 us  [on_device(): pl.pallas_call(functools.partial(kernel, dims), out_shape=(jax.ShapeDtype...]
where the time goes in v1:
time: 175 us; the launch traced here: 174 us
  Pallas kernels  170 us (97%)
  other arithmetic  2.41 us (1%)
    pallas_call x1, Pallas kernels, on_device(): pl.pallas_call(functools.partial(kernel, dims), out_shape=(jax.ShapeDtype...  170 us

profile of v1, /device:TPU:0, one launch (start us, length us, event | category | flops | bytes accessed | tf_op | source)
XLA Modules:
  0.0 174.4 jit_solution(1135892944009160451)
XLA Ops:
  0.6 0.0 copy-start
  0.6 0.9 copy-done
  1.5 0.0 copy-start.1
  1.5 0.7 copy-done.1
  2.2 0.0 copy-start.2
  2.2 0.0 copy-start.3
  2.2 169.6 %reduce_gradient.1 = (f32[2,16,14336]{2,1,0:T(8,128)S(1)}, f32[8,128]{1,0:T(8,128)S(1)}) custom-call(bf16[2,128,256]{2,1,0:T(8,128)(2,1)S(1)} %bitcast.25, bf16[2,128,14336]{2,1,0:T(8,128)(2,1)} %bitcast.26, s32[2,1,2]{2,1,0:T(1,128)S(1)} %copy-done.1), custom_call_target="tpu_custom_call" | custom-call | tf_op jit(solution)/shard_map/reduce_gradient/pallas_call | solution.py:331
  171.8 0.1 slice_reduce_fusion
  171.9 0.0 copy-done.2
  172.0 0.0 copy-done.3
  172.0 2.4 %fusion.1 = (f32[2,1,16,14336]{3,2,1,0:T(8,128)}, f32[2,1,16,14336]{3,2,1,0:T(8,128)}) fusion(f32[2,1,16,14336]{3,2,1,0:T(8,128)S(1)} %copy-done.2, f32[2]{0:T(128)S(1)} %get-tuple-element.10, f32[2,16,14336]{2,1,0:T(8,128)S(1)} %get-tuple-element.5, f32[2]{0:T(128)S(1)} %get-tuple-element.11, f32[2,1,16,14336]{3,2,1,0:T(8,128)S(1)} %copy-done.3), kind=kLoop, calls=%fused_computation.3 | loop fusion | flops 2293760 | bytes 9175056
Async XLA Ops:
  0.6 0.9 copy-start
  1.5 0.7 copy-start.1
  2.2 169.7 %copy-start.2 = (f32[2,1,16,14336]{3,2,1,0:T(8,128)S(1)}, f32[2,1,16,14336]{3,2,1,0:T(8,128)}, u32[]{:S(2)}) copy-start(f32[2,1,16,14336]{3,2,1,0:T(8,128)} %param.8) | copy-start | bytes 5505028
  2.2 169.7 %copy-start.3 = (f32[2,1,16,14336]{3,2,1,0:T(8,128)S(1)}, f32[2,1,16,14336]{3,2,1,0:T(8,128)}, u32[]{:S(2)}) copy-start(f32[2,1,16,14336]{3,2,1,0:T(8,128)} %param.7) | copy-start | bytes 5505028

commit v2 on v1

v2 whole, which is shorter than its diff:
```python
import functools

import jax
import jax.numpy as jnp
from jax import lax
from jax.experimental import pallas as pl
from jax.experimental.pallas import tpu as pltpu
from jax.sharding import PartitionSpec as P

step_size = 0.5
clip_level = 1.0
CORES = 2
SLOTS = 4
LAG = 6
HOP = 3
HOP_LATE = 3
TAIL = 6
AHEAD = 6
RING = 8
CUT = 0
FEWER = 0
PIECES = 28
MESH = pl.DeviceIdType.MESH


def kernel(
    dims, act_hbm, cot_hbm, cnt_hbm, out_ref, stat_ref,
    acts, cnt, turned, rows_ref, cot, merged, from_y, from_z, from_zx, late_y, staged,
    squares, counted, seen, message, gathered,
    act_sem, cnt_sem, cot_sem, core_send, core_recv, y_send, y_recv, tail_send, tail_recv, z_send, z_recv,
    zx_send, zx_recv, late_send, late_recv, cnt_send, cnt_recv, all_send, all_recv,
):
    line, experts, shards, layers, per_layer, width, rows, numel, period, lates, ring, late_ring, y_ring = dims
    group = line * shards
    half = line * rows
    chunks = layers * per_layer
    first_tail = chunks - TAIL
    z, e, s = lax.axis_index("dp"), lax.axis_index("expert"), lax.axis_index("shard")
    y, c = s // CORES, s % CORES
    me = z * shards + s
    core_peer = {"shard": y * CORES + (1 - c)}
    y_peer = {"shard": (1 - y) * CORES + c}
    own, other = y * half, (1 - y) * half

    def place(k):
        return k // per_layer, k % per_layer

    def columns(q):
        return pl.ds(pl.multiple_of(q * width, 128), width)

    def fetch(k):
        layer, q = place(k)
        return pltpu.make_async_copy(
            cot_hbm.at[layer, :, columns(q)], cot.at[k % RING], cot_sem.at[k % RING]
        )

    act_copy = pltpu.make_async_copy(act_hbm, acts, act_sem)
    cnt_fetch = pltpu.make_async_copy(cnt_hbm, cnt, cnt_sem)
    act_copy.start()
    fetch(0).start()

    def group_peer(d):
        p = lax.rem(me + d, group)
        return p, {"dp": p // shards, "shard": p % shards}

    def remote(src, dst, send, recv, device):
        return pltpu.make_async_remote_copy(
            src_ref=src, dst_ref=dst, send_sem=send, recv_sem=recv,
            device_id=device, device_id_type=MESH,
        )

    barrier = pltpu.get_barrier_semaphore()
    for d in range(1, group):
        pl.semaphore_signal(barrier, inc=1, device_id=group_peer(d)[1], device_id_type=MESH)
    for d in range(1, experts):
        pl.semaphore_signal(
            barrier, inc=1, device_id={"expert": lax.rem(e + d, experts)}, device_id_type=MESH
        )

    for k in range(1, min(AHEAD, chunks)):
        fetch(k).start()
    cnt_fetch.start()

    def turn(layer):
        across = acts[layer].astype(jnp.float32).T
        for b in range(line):
            for h in range(shards // CORES):
                for core in range(CORES):
                    at = ((b * (shards // CORES) + h) * CORES + core) * rows
                    to = (h * line + b) * rows
                    turned[core, to:to + rows, :] = across[at:at + rows]
        for core in range(CORES):
            rows_ref[layer, core] = turned[core].astype(rows_ref.dtype)

    act_copy.wait()
    turn(0)
    pl.semaphore_wait(barrier, group + experts - 2)

    row = lax.broadcasted_iota(jnp.int32, counted.shape, 0)
    lane = lax.broadcasted_iota(jnp.int32, counted.shape, 1)

    def count_copy(d, sender):
        return remote(
            counted, seen.at[sender], cnt_send.at[d], cnt_recv.at[sender],
            {"expert": lax.rem(e + d, experts)},
        )

    def prepare():
        for layer in range(1, layers):
            turn(layer)
        cnt_fetch.wait()
        tile = jnp.zeros(counted.shape, jnp.float32)
        for layer in range(layers):
            for p in range(experts):
                here = (row == layers + layer) & (lane == p)
                tile = jnp.where(here, cnt[layer, 0, p].astype(jnp.float32), tile)
        counted[...] = tile
        squares[...] = jnp.zeros_like(squares)
        for d in range(1, experts):
            count_copy(d, e).start()

    def is_late(k):
        return (k % period == 1) & (k < period * lates)

    def late_chunk(j):
        return j * period + 1

    def when_chunk(k, body):
        pl.when((k >= 0) & (k < chunks))(lambda: body(k))

    def when_early(k, body):
        when_chunk(k, lambda k: pl.when(jnp.logical_not(is_late(k)))(lambda: body(k)))

    def when_chain(k, body):
        when_early(k, lambda k: pl.when(k < first_tail)(lambda: body(k)))

    def when_tail(k, body):
        pl.when((k >= first_tail) & (k < chunks))(lambda: body(k))

    def when_late(k, body):
        when_chunk(k, lambda k: pl.when(is_late(k))(lambda: body(k)))

    def core_copy(k):
        return remote(
            staged.at[k % SLOTS], merged.at[k], core_send.at[k % SLOTS], core_recv.at[k % SLOTS], core_peer
        )

    def y_copy(k):
        return remote(
            merged.at[k, pl.ds(pl.multiple_of(other, 8), half)], from_y.at[k],
            y_send.at[k % y_ring], y_recv.at[k % y_ring], y_peer,
        )

    def late_copy(k):
        j = k // period
        return remote(
            merged.at[k, pl.ds(pl.multiple_of(other + z * rows, 8), rows)], late_y.at[j],
            late_send.at[j], late_recv.at[j], y_peer,
        )

    def product(k, core):
        layer, _ = place(k)
        return jnp.dot(
            rows_ref[layer, core], cot[k % RING], preferred_element_type=jnp.float32
        )

    def stage_partner(k):
        pl.when(k >= SLOTS)(lambda: core_copy(k - SLOTS).wait_send())
        fetch(k).wait()
        staged[k % SLOTS] = product(k, 1 - c)
        core_copy(k).start()

    def merge_core(k):
        core_copy(k).wait_recv()
        merged[k] = merged[k] + product(k, c)
        when_chain(k, lambda k: y_copy(k).start())
        when_tail(k, lambda k: other_blocks(lambda b: tail_copy(k, b).start()))

    def tail_copy(k, b):
        i = k - first_tail
        at = pl.ds(pl.multiple_of(other + b * rows, 8), rows)
        return remote(
            merged.at[k, at], from_y.at[k, b * rows:(b + 1) * rows],
            tail_send.at[i, b], tail_recv.at[i, b], y_peer,
        )

    def other_blocks(body):
        for b in range(line):
            pl.when(z != b)(lambda: body(b))

    def own_block(body):
        for b in range(line):
            pl.when(z == b)(lambda: body(b))

    def merge_y(k):
        y_copy(k).wait_recv()
        at = pl.ds(pl.multiple_of(own, 8), half)
        merged[k, at, :] = merged[k, at, :] + from_y[k]

    def merge_block(k, b):
        tail_copy(k, b).wait_recv()
        at = pl.ds(pl.multiple_of(own + b * rows, 8), rows)
        merged[k, at, :] = merged[k, at, :] + from_y[k, b * rows:(b + 1) * rows, :]

    def merge_tail(k):
        other_blocks(lambda b: merge_block(k, b))

    def block(k, base, b):
        return merged.at[k, pl.ds(pl.multiple_of(base + b * rows, 8), rows)]

    def z_copy(k, base, b, slot, device, late):
        if late is None:
            return remote(
                block(k, base, b), from_z.at[k, slot], z_send.at[k % ring, b],
                z_recv.at[k % ring, slot], device,
            )
        j = k // period
        n = late * (line + 1) + slot
        return remote(
            block(k, base, b), from_zx.at[j, n], zx_send.at[j % late_ring, late * line + b],
            zx_recv.at[j % late_ring, n], device,
        )

    def arrived(k, slot, late):
        if late is None:
            return from_z[k, slot]
        return from_zx[k // period, late * (line + 1) + slot]

    def add_arrived(k, base, b, slot, late):
        z_copy(k, base, b, slot, {"dp": z}, late).wait_recv()
        ref = block(k, base, b)
        ref[...] = ref[...] + arrived(k, slot, late)

    def send_right(k, base, b, late):
        @pl.when(z < b)
        def _():
            pl.when(z > 0)(lambda: add_arrived(k, base, b, b + 1, late))
            z_copy(k, base, b, b + 1, {"dp": z + 1}, late).start()

    def send_left(k, base, b, late):
        @pl.when(z > b)
        def _():
            pl.when(z < line - 1)(lambda: add_arrived(k, base, b, b, late))
            z_copy(k, base, b, b, {"dp": z - 1}, late).start()

    def to_right(k, base, late):
        for b in reversed(range(1, line)):
            send_right(k, base, b, late)

    def to_left(k, base, late):
        for b in range(line - 1):
            send_left(k, base, b, late)

    def far_right(k):
        for b in reversed(range(2, line)):
            pl.when(z + 1 < b)(lambda: send_right(k, own, b, None))

    def far_left(k):
        for b in range(line - 2):
            pl.when(z - 1 > b)(lambda: send_left(k, own, b, None))

    def near_right(k, _):
        for b in range(1, line):
            pl.when(z + 1 == b)(lambda: send_right(k, own, b, None))

    def near_left(k, _):
        for b in range(line - 1):
            pl.when(z - 1 == b)(lambda: send_left(k, own, b, None))

    def both_halves(one):
        def body(k):
            one(k, other, 0)
            one(k, own, 1)
        return body

    def own_half(one):
        return lambda k: one(k, own, None)

    def put(k, values):
        layer, q = place(k)
        out_ref[layer, :, columns(q)] = values
        squares[layer] = squares[layer] + values * values

    def gather_block(k, base, late):
        pl.when(z > 0)(lambda: add_arrived(k, base, z, z + 1, late))
        pl.when(z < line - 1)(lambda: add_arrived(k, base, z, z, late))

    def finish_early(k):
        gather_block(k, own, None)
        put(k, block(k, own, z)[...])

    def finish_tail(k, _):
        own_block(lambda b: merge_block(k, b))
        finish_early(k)

    def finish_late(k):
        gather_block(k, other, 0)
        gather_block(k, own, 1)

    back = line - 1 - z
    far = jnp.maximum(z, back)

    def on_tail(body):
        return lambda: lax.fori_loop(first_tail, chunks, body, None)

    def step(t, _):
        pl.when(t + AHEAD < chunks)(lambda: fetch(t + AHEAD).start())
        when_chunk(t, stage_partner)
        when_chunk(t - 1, merge_core)
        when_late(t - 1 - HOP_LATE * z, both_halves(to_right))
        when_late(t - 1 - HOP_LATE * back, both_halves(to_left))
        when_late(t - 1 - HOP_LATE * far, finish_late)
        pl.when(t == 2)(prepare)
        when_chain(t - LAG, merge_y)
        when_tail(t - LAG, merge_tail)
        when_chain(t - LAG - HOP * z, own_half(to_right))
        when_chain(t - LAG - HOP * back, own_half(to_left))
        when_chain(t - LAG - HOP * far, finish_early)
        when_tail(t - LAG - HOP * z, far_right)
        when_tail(t - LAG - HOP * back, far_left)
        pl.when(t == chunks - 1 + LAG + HOP * z)(on_tail(near_right))
        pl.when(t == chunks - 1 + LAG + HOP * back)(on_tail(near_left))
        pl.when(t == start_late)(send_lates)
        when_chain(t - LAG - 1, drain_y)
        when_late(t - late_behind, drain_late)
        when_chain(t - behind, drain_z)
        return 0

    late_end = late_chunk(lates - 1) + 1 + HOP_LATE * (line - 1)
    start_late = max(chunks, late_end)
    behind = LAG + HOP * (line - 1) + 3
    late_behind = HOP_LATE * (line - 1) + 3
    steps = max(chunks + LAG + HOP * (line - 1), start_late + 1)

    def send_late(j, _):
        late_copy(late_chunk(j)).start()

    def send_own(k, _):
        own_block(lambda b: tail_copy(k, b).start())

    def send_lates():
        lax.fori_loop(0, lates, send_late, None)
        lax.fori_loop(first_tail, chunks, send_own, None)

    def drain_y(k):
        y_copy(k).wait_send()

    def drain_z(k):
        for b in range(line):
            pl.when(z != b)(lambda: z_copy(k, own, b, b, {"dp": z}, None).wait_send())

    def drain_late(k):
        for b in range(line):
            pl.when(z != b)(lambda: z_copy(k, other, b, b, {"dp": z}, 0).wait_send())
            pl.when(z != b)(lambda: z_copy(k, own, b, b, {"dp": z}, 1).wait_send())

    lax.fori_loop(0, steps, step, 0)

    def add_late(j, _):
        k = late_chunk(j)
        late_copy(k).wait_recv()
        put(k, block(k, own, z)[...] + late_y[j])
        return 0

    lax.fori_loop(0, lates, add_late, 0)
    lax.fori_loop(first_tail, chunks, finish_tail, None)

    totals = counted[...]
    for d in range(1, experts):
        sender = lax.rem(e + d, experts)
        count_copy(d, sender).wait_recv()
        totals = totals + seen[sender]
    for layer in range(layers):
        share = jnp.sum(jnp.sum(squares[layer], axis=0, keepdims=True), axis=1, keepdims=True)
        totals = jnp.where(row == layer, share, totals)
    message[...] = totals
    gathered[me] = totals

    def all_copy(d, sender):
        return remote(
            message, gathered.at[sender], all_send.at[d], all_recv.at[sender], group_peer(d)[1]
        )

    for d in range(1, group):
        all_copy(d, me).start()
    def drain_rest(k, _):
        drain_z(k)
        for b in range(line):
            tail_copy(k, b).wait_send()

    for k in range(chunks - min(SLOTS, chunks), chunks):
        core_copy(k).wait_send()
    lax.fori_loop(
        steps - behind, first_tail, lambda k, _: when_chain(k, drain_z), None
    )
    lax.fori_loop(first_tail, chunks, drain_rest, None)
    lax.fori_loop(
        0, lates, lambda j, _: late_copy(late_chunk(j)).wait_send(), None
    )

    for d in range(1, group):
        all_copy(d, group_peer(d)[0]).wait_recv()
    total = gathered[0]
    for p in range(1, group):
        total = total + gathered[p]
    stats = jnp.zeros_like(total)
    for layer in range(layers):
        loads = total[layers + layer:layers + layer + 1, :]
        spot = lane[:1]
        own_load = jnp.sum(jnp.where(spot == e, loads, 0.0), axis=1, keepdims=True)
        mean_load = jnp.sum(jnp.where(spot < experts, loads, 0.0), axis=1, keepdims=True) / experts
        root_mean = jnp.sqrt(total[layer:layer + 1, :1] / numel)
        factor = (
            step_size * (own_load / mean_load) * clip_level / jnp.maximum(root_mean, clip_level)
        )
        beta = own_load / (own_load + mean_load)
        stats = jnp.where(row == layer, factor, stats)
        stats = jnp.where(row == layers + layer, beta, stats)
    stat_ref[...] = stats

    for d in range(1, group):
        all_copy(d, me).wait_send()
    for d in range(1, experts):
        count_copy(d, e).wait_send()


def on_device(sizes, activations, out_grads, weights, shadow, counts):
    line, experts, shards = sizes
    layers, _, tokens, all_rows = activations.shape
    ff, rows = out_grads.shape[3], weights.shape[2]
    assert shards == 2 * CORES and 2 * layers <= 8
    units = ff // 128
    per_layer = next(
        p for p in range(PIECES, units + 1) if units % p == 0 and units // p % 2 == 0
    )
    width = ff // per_layer
    chunks = layers * per_layer
    half = line * rows
    group = line * shards
    period = max(2, 2 * (line - 1))
    lates = chunks // period - FEWER
    period = max(2, period - CUT)
    ring = HOP * (line - 1) + HOP + 4
    y_ring = 2 * LAG + 2
    assert (lates - 1) * period + 1 < chunks - TAIL
    late_ring = min(lates, -(-(HOP_LATE * (line - 1) + HOP + 6) // period))
    f32 = jnp.float32
    dma = pltpu.SemaphoreType.DMA
    vmem = pl.BlockSpec(memory_space=pltpu.VMEM)
    hbm = pl.BlockSpec(memory_space=pltpu.HBM)
    dims = (
        line, experts, shards, layers, per_layer, width, rows, all_rows * ff, period, lates, ring,
        late_ring, y_ring,
    )
    summed, stats = pl.pallas_call(
        functools.partial(kernel, dims),
        out_shape=(
            jax.ShapeDtypeStruct((layers, rows, ff), f32), jax.ShapeDtypeStruct((8, 128), f32)
        ),
        in_specs=[hbm] * 3,
        out_specs=(vmem, vmem),
        scratch_shapes=[
            pltpu.VMEM((layers, tokens, all_rows), activations.dtype),
            pltpu.SMEM((layers, 1, experts), jnp.int32),
            pltpu.VMEM((CORES, 2 * half, tokens), f32),
            pltpu.VMEM((layers, CORES, 2 * half, tokens), activations.dtype),
            pltpu.VMEM((RING, tokens, width), out_grads.dtype),
            pltpu.VMEM((chunks, 2 * half, width), f32),
            pltpu.VMEM((chunks, half, width), f32),
            pltpu.VMEM((chunks, line + 1, rows, width), f32),
            pltpu.VMEM((lates, 2 * (line + 1), rows, width), f32),
            pltpu.VMEM((lates, rows, width), f32),
            pltpu.VMEM((SLOTS, 2 * half, width), f32),
            pltpu.VMEM((layers, rows, width), f32),
            pltpu.VMEM((8, 128), f32),
            pltpu.VMEM((experts, 8, 128), f32),
            pltpu.VMEM((8, 128), f32),
            pltpu.VMEM((group, 8, 128), f32),
            dma, dma, dma((RING,)),
            dma((SLOTS,)), dma((SLOTS,)), dma((y_ring,)), dma((y_ring,)),
            dma((TAIL, line)), dma((TAIL, line)),
            dma((ring, line)), dma((ring, line + 1)),
            dma((late_ring, 2 * line)), dma((late_ring, 2 * (line + 1))),
            dma((lates,)), dma((lates,)), dma((experts,)), dma((experts,)),
            dma((group,)), dma((group,)),
        ],
        compiler_params=pltpu.CompilerParams(
            collective_id=0, has_side_effects=True, vmem_limit_bytes=46 * 1024 * 1024
        ),
        name="reduce_gradient",
    )(
        pltpu.with_memory_space_constraint(activations[:, 0], pltpu.HBM), out_grads[:, 0],
        pltpu.with_memory_space_constraint(counts, pltpu.HBM),
    )
    factor = stats[:layers, 0][:, None, None]
    beta = stats[layers:2 * layers, 0][:, None, None]
    updated = weights[:, 0] - factor * summed
    previous = shadow[:, 0]
    return updated[:, None], (previous + beta * (updated - previous))[:, None]


def solution(mesh):
    rows = P(None, "expert", ("dp", "shard"), None)
    in_specs = (rows, rows, rows, rows, P(None, ("dp", "expert", "shard"), None))
    sizes = tuple(mesh.shape[a] for a in ("dp", "expert", "shard"))
    return jax.shard_map(
        functools.partial(on_device, sizes), mesh=mesh, in_specs=in_specs,
        out_specs=(rows, rows), check_vma=False,
    )
```

time: 175 us -> 160 us (0.914)
  Pallas kernels: 170 us -> 156 us
    pallas_call x1, Pallas kernels: 170 us -> 156 us  [on_device(): pl.pallas_call(functools.partial(kernel, dims), out_shape=(jax.ShapeDtype...]
where the time goes in v2:
time: 160 us; the launch traced here: 159 us
  Pallas kernels  156 us (98%)
  other arithmetic  2.41 us (2%)
    pallas_call x1, Pallas kernels, on_device(): pl.pallas_call(functools.partial(kernel, dims), out_shape=(jax.ShapeDtype...  156 us

profile of v2, /device:TPU:0, one launch (start us, length us, event | category | flops | bytes accessed | tf_op | source)
XLA Modules:
  0.0 159.5 jit_solution(8556807665657734511)
XLA Ops:
  0.6 0.0 copy-start
  0.6 0.0 copy-start.1
  0.7 156.2 %reduce_gradient.1 = (f32[2,16,14336]{2,1,0:T(8,128)S(1)}, f32[8,128]{1,0:T(8,128)S(1)}) custom-call(bf16[2,128,256]{2,1,0:T(8,128)(2,1)} %bitcast.26, bf16[2,128,14336]{2,1,0:T(8,128)(2,1)} %bitcast.25, s32[2,1,2]{2,1,0:T(1,128)} %cnt_hbm.1), custom_call_target="tpu_custom_call" | custom-call | tf_op jit(solution)/shard_map/reduce_gradient/pallas_call | solution.py:455
  156.9 0.1 slice_reduce_fusion
  157.0 0.0 copy-done
  157.0 0.0 copy-done.1
  157.1 2.4 %fusion.1 = (f32[2,1,16,14336]{3,2,1,0:T(8,128)}, f32[2,1,16,14336]{3,2,1,0:T(8,128)}) fusion(f32[2,1,16,14336]{3,2,1,0:T(8,128)S(1)} %copy-done, f32[2]{0:T(128)S(1)} %get-tuple-element.10, f32[2,16,14336]{2,1,0:T(8,128)S(1)} %get-tuple-element.5, f32[2]{0:T(128)S(1)} %get-tuple-element.11, f32[2,1,16,14336]{3,2,1,0:T(8,128)S(1)} %copy-done.1), kind=kLoop, calls=%fused_computation.3 | loop fusion | flops 2293760 | bytes 9175056
Async XLA Ops:
  0.6 156.4 %copy-start = (f32[2,1,16,14336]{3,2,1,0:T(8,128)S(1)}, f32[2,1,16,14336]{3,2,1,0:T(8,128)}, u32[]{:S(2)}) copy-start(f32[2,1,16,14336]{3,2,1,0:T(8,128)} %param.8) | copy-start | bytes 5505028
  0.6 156.4 %copy-start.1 = (f32[2,1,16,14336]{3,2,1,0:T(8,128)S(1)}, f32[2,1,16,14336]{3,2,1,0:T(8,128)}, u32[]{:S(2)}) copy-start(f32[2,1,16,14336]{3,2,1,0:T(8,128)} %param.7) | copy-start | bytes 5505028

commit v3 on v2

--- a/solution.py
+++ b/solution.py
@@ -70,13 +70,15 @@
         )
 
     barrier = pltpu.get_barrier_semaphore()
-    for d in range(1, group):
-        pl.semaphore_signal(barrier, inc=1, device_id=group_peer(d)[1], device_id_type=MESH)
+    def greet(device):
+        pl.semaphore_signal(barrier, inc=1, device_id=device, device_id_type=MESH)
+
+    greet(core_peer)
+    greet(y_peer)
+    pl.when(z > 0)(lambda: greet({"dp": z - 1}))
+    pl.when(z < line - 1)(lambda: greet({"dp": z + 1}))
     for d in range(1, experts):
-        pl.semaphore_signal(
-            barrier, inc=1, device_id={"expert": lax.rem(e + d, experts)}, device_id_type=MESH
-        )
-
+        greet({"expert": lax.rem(e + d, experts)})
     for k in range(1, min(AHEAD, chunks)):
         fetch(k).start()
     cnt_fetch.start()
@@ -94,7 +96,8 @@
 
     act_copy.wait()
     turn(0)
-    pl.semaphore_wait(barrier, group + experts - 2)
+    ends = (z == 0).astype(jnp.int32) + (z == line - 1).astype(jnp.int32)
+    pl.semaphore_wait(barrier, experts + 3 - ends)
 
     row = lax.broadcasted_iota(jnp.int32, counted.shape, 0)
     lane = lax.broadcasted_iota(jnp.int32, counted.shape, 1)
@@ -155,7 +158,7 @@
         j = k // period
         return remote(
             merged.at[k, pl.ds(pl.multiple_of(other + z * rows, 8), rows)], late_y.at[j],
-            late_send.at[j], late_recv.at[j], y_peer,
+            late_send, late_recv, y_peer,
         )
 
     def product(k, core):
@@ -181,7 +184,7 @@
         at = pl.ds(pl.multiple_of(other + b * rows, 8), rows)
         return remote(
             merged.at[k, at], from_y.at[k, b * rows:(b + 1) * rows],
-            tail_send.at[i, b], tail_recv.at[i, b], y_peer,
+            tail_send.at[i], tail_recv.at[i, b], y_peer,
         )
 
     def other_blocks(body):
@@ -211,13 +214,13 @@
     def z_copy(k, base, b, slot, device, late):
         if late is None:
             return remote(
-                block(k, base, b), from_z.at[k, slot], z_send.at[k % ring, b],
+                block(k, base, b), from_z.at[k, slot], z_send.at[k % ring],
                 z_recv.at[k % ring, slot], device,
             )
         j = k // period
         n = late * (line + 1) + slot
         return remote(
-            block(k, base, b), from_zx.at[j, n], zx_send.at[j % late_ring, late * line + b],
+            block(k, base, b), from_zx.at[j, n], zx_send.at[j % late_ring],
             zx_recv.at[j % late_ring, n], device,
         )
 
@@ -345,23 +348,27 @@
     def drain_y(k):
         y_copy(k).wait_send()
 
+    def sent(k, count, semaphore):
+        ref = merged.at[k, 0:count * rows]
+        remote(ref, ref, semaphore, semaphore, y_peer).wait_send()
+
     def drain_z(k):
-        for b in range(line):
-            pl.when(z != b)(lambda: z_copy(k, own, b, b, {"dp": z}, None).wait_send())
+        sent(k, line - 1, z_send.at[k % ring])
 
     def drain_late(k):
-        for b in range(line):
-            pl.when(z != b)(lambda: z_copy(k, other, b, b, {"dp": z}, 0).wait_send())
-            pl.when(z != b)(lambda: z_copy(k, own, b, b, {"dp": z}, 1).wait_send())
+        sent(k, 2 * (line - 1), zx_send.at[k // period % late_ring])
 
     lax.fori_loop(0, steps, step, 0)
+
+    def all_late():
+        return remote(late_y, late_y, late_send, late_recv, y_peer)
 
     def add_late(j, _):
         k = late_chunk(j)
-        late_copy(k).wait_recv()
         put(k, block(k, own, z)[...] + late_y[j])
         return 0
 
+    all_late().wait_recv()
     lax.fori_loop(0, lates, add_late, 0)
     lax.fori_loop(first_tail, chunks, finish_tail, None)
 
@@ -378,15 +385,14 @@
 
     def all_copy(d, sender):
         return remote(
-            message, gathered.at[sender], all_send.at[d], all_recv.at[sender], group_peer(d)[1]
+            message, gathered.at[sender], all_send, all_recv, group_peer(d)[1]
         )
 
     for d in range(1, group):
         all_copy(d, me).start()
     def drain_rest(k, _):
         drain_z(k)
-        for b in range(line):
-            tail_copy(k, b).wait_send()
+        sent(k, line, tail_send.at[k - first_tail])
 
     for k in range(chunks - min(SLOTS, chunks), chunks):
         core_copy(k).wait_send()
@@ -394,12 +400,13 @@
         steps - behind, first_tail, lambda k, _: when_chain(k, drain_z), None
     )
     lax.fori_loop(first_tail, chunks, drain_rest, None)
-    lax.fori_loop(
-        0, lates, lambda j, _: late_copy(late_chunk(j)).wait_send(), None
-    )
-
-    for d in range(1, group):
-        all_copy(d, group_peer(d)[0]).wait_recv()
+    all_late().wait_send()
+
+    def all_others():
+        others = gathered.at[0:group - 1]
+        return remote(others, others, all_send, all_recv, y_peer)
+
+    all_others().wait_recv()
     total = gathered[0]
     for p in range(1, group):
         total = total + gathered[p]
@@ -418,8 +425,7 @@
         stats = jnp.where(row == layers + layer, beta, stats)
     stat_ref[...] = stats
 
-    for d in range(1, group):
-        all_copy(d, me).wait_send()
+    all_others().wait_send()
     for d in range(1, experts):
         count_copy(d, e).wait_send()
 
@@ -440,7 +446,7 @@
     period = max(2, 2 * (line - 1))
     lates = chunks // period - FEWER
     period = max(2, period - CUT)
-    ring = HOP * (line - 1) + HOP + 4
+    ring = HOP * (line - 1) + HOP + 3
     y_ring = 2 * LAG + 2
     assert (lates - 1) * period + 1 < chunks - TAIL
     late_ring = min(lates, -(-(HOP_LATE * (line - 1) + HOP + 6) // period))
@@ -478,11 +484,10 @@
             pltpu.VMEM((group, 8, 128), f32),
             dma, dma, dma((RING,)),
             dma((SLOTS,)), dma((SLOTS,)), dma((y_ring,)), dma((y_ring,)),
-            dma((TAIL, line)), dma((TAIL, line)),
-            dma((ring, line)), dma((ring, line + 1)),
-            dma((late_ring, 2 * line)), dma((late_ring, 2 * (line + 1))),
-            dma((lates,)), dma((lates,)), dma((experts,)), dma((experts,)),
-            dma((group,)), dma((group,)),
+            dma((TAIL,)), dma((TAIL, line)),
+            dma((ring,)), dma((ring, line + 1)),
+            dma((late_ring,)), dma((late_ring, 2 * (line + 1))),
+            dma, dma, dma((experts,)), dma((experts,)), dma, dma,
         ],
         compiler_params=pltpu.CompilerParams(
             collective_id=0, has_side_effects=True, vmem_limit_bytes=46 * 1024 * 1024

time: 160 us -> 158 us (0.988)
  Pallas kernels: 156 us -> 154 us
    pallas_call x1, Pallas kernels: 156 us -> 154 us  [on_device(): pl.pallas_call(functools.partial(kernel, dims), out_shape=(jax.ShapeDtype...]
where the time goes in v3:
time: 158 us
  Pallas kernels  154 us (97%)
  other arithmetic  2.41 us (2%)
    pallas_call x1, Pallas kernels, on_device(): pl.pallas_call(functools.partial(kernel, dims), out_shape=(jax.ShapeDtype...  154 us

profile of v3, /device:TPU:0, one launch (start us, length us, event | category | flops | bytes accessed | tf_op | source)
XLA Modules:
  0.0 157.7 jit_solution(7998622238633739518)
XLA Ops:
  0.6 0.0 copy-start
  0.6 0.0 copy-start.1
  0.7 154.4 %reduce_gradient.1 = (f32[2,16,14336]{2,1,0:T(8,128)S(1)}, f32[8,128]{1,0:T(8,128)S(1)}) custom-call(bf16[2,128,256]{2,1,0:T(8,128)(2,1)} %bitcast.26, bf16[2,128,14336]{2,1,0:T(8,128)(2,1)} %bitcast.25, s32[2,1,2]{2,1,0:T(1,128)} %cnt_hbm.1), custom_call_target="tpu_custom_call" | custom-call | tf_op jit(solution)/shard_map/reduce_gradient/pallas_call | solution.py:461
  155.1 0.1 slice_reduce_fusion
  155.2 0.0 copy-done
  155.3 0.0 copy-done.1
  155.3 2.4 %fusion.1 = (f32[2,1,16,14336]{3,2,1,0:T(8,128)}, f32[2,1,16,14336]{3,2,1,0:T(8,128)}) fusion(f32[2,1,16,14336]{3,2,1,0:T(8,128)S(1)} %copy-done, f32[2]{0:T(128)S(1)} %get-tuple-element.10, f32[2,16,14336]{2,1,0:T(8,128)S(1)} %get-tuple-element.5, f32[2]{0:T(128)S(1)} %get-tuple-element.11, f32[2,1,16,14336]{3,2,1,0:T(8,128)S(1)} %copy-done.1), kind=kLoop, calls=%fused_computation.3 | loop fusion | flops 2293760 | bytes 9175056
Async XLA Ops:
  0.6 154.6 %copy-start = (f32[2,1,16,14336]{3,2,1,0:T(8,128)S(1)}, f32[2,1,16,14336]{3,2,1,0:T(8,128)}, u32[]{:S(2)}) copy-start(f32[2,1,16,14336]{3,2,1,0:T(8,128)} %param.8) | copy-start | bytes 5505028
  0.6 154.6 %copy-start.1 = (f32[2,1,16,14336]{3,2,1,0:T(8,128)S(1)}, f32[2,1,16,14336]{3,2,1,0:T(8,128)}, u32[]{:S(2)}) copy-start(f32[2,1,16,14336]{3,2,1,0:T(8,128)} %param.7) | copy-start | bytes 5505028

commit v4 on v3

--- a/solution.py
+++ b/solution.py
@@ -15,6 +15,7 @@
 HOP = 3
 HOP_LATE = 3
 TAIL = 6
+SPLIT = 4
 AHEAD = 6
 RING = 8
 CUT = 0
@@ -428,6 +429,30 @@
     all_others().wait_send()
     for d in range(1, experts):
         count_copy(d, e).wait_send()
+
+
+def update(
+    layers, ff, stats, summed, weights, shadow, new_weights, new_shadow, updated, smoothed,
+    weights_sem, shadow_sem,
+):
+    width = ff // SPLIT
+    for layer in range(layers):
+        factor = stats[layer:layer + 1, :1]
+        beta = stats[layers + layer:layers + layer + 1, :1]
+        for p in range(SPLIT):
+            at = slice(p * width, (p + 1) * width)
+            fresh = weights[layer, :, at] - factor * summed[layer, :, at]
+            previous = shadow[layer, :, at]
+            updated[layer, :, at] = fresh
+            smoothed[layer, :, at] = previous + beta * (fresh - previous)
+            pltpu.make_async_copy(
+                updated.at[layer, :, at], new_weights.at[layer, :, at], weights_sem
+            ).start()
+            pltpu.make_async_copy(
+                smoothed.at[layer, :, at], new_shadow.at[layer, :, at], shadow_sem
+            ).start()
+    pltpu.make_async_copy(updated, new_weights, weights_sem).wait()
+    pltpu.make_async_copy(smoothed, new_shadow, shadow_sem).wait()
 
 
 def on_device(sizes, activations, out_grads, weights, shadow, counts):
@@ -497,11 +522,18 @@
         pltpu.with_memory_space_constraint(activations[:, 0], pltpu.HBM), out_grads[:, 0],
         pltpu.with_memory_space_constraint(counts, pltpu.HBM),
     )
-    factor = stats[:layers, 0][:, None, None]
-    beta = stats[layers:2 * layers, 0][:, None, None]
-    updated = weights[:, 0] - factor * summed
-    previous = shadow[:, 0]
-    return updated[:, None], (previous + beta * (updated - previous))[:, None]
+    updated, smoothed = pl.pallas_call(
+        functools.partial(update, layers, ff),
+        out_shape=(jax.ShapeDtypeStruct((layers, rows, ff), f32),) * 2,
+        in_specs=[vmem] * 4,
+        out_specs=(hbm, hbm),
+        scratch_shapes=[
+            pltpu.VMEM((layers, rows, ff), f32), pltpu.VMEM((layers, rows, ff), f32), dma, dma
+        ],
+        compiler_params=pltpu.CompilerParams(vmem_limit_bytes=12 * 1024 * 1024),
+        name="update",
+    )(stats, summed, weights[:, 0], shadow[:, 0])
+    return updated[:, None], smoothed[:, None]
 
 
 def solution(mesh):

time: 158 us -> 157 us (level)
  other arithmetic: 2.41 us -> 0 us
  Pallas kernels: 154 us -> 156 us
    unnamed x1 -> x0, other arithmetic: 2.41 us -> none
    pallas_call x0 -> x1, Pallas kernels: none -> 1.94 us  [on_device(): pl.pallas_call(functools.partial(update, layers, ff), out_shape=(jax.Shap...]
where the time goes in v4:
time: 157 us
  Pallas kernels  156 us (99%)
    pallas_call x1, Pallas kernels, on_device(): pl.pallas_call(functools.partial(kernel, dims), out_shape=(jax.ShapeDtype...  154 us

profile of v4, /device:TPU:0, one launch (start us, length us, event | category | flops | bytes accessed | tf_op | source)
XLA Modules:
  0.0 157.1 jit_solution(2759497079450484332)
XLA Ops:
  0.6 0.0 copy-start
  0.6 0.0 copy-start.1
  0.7 154.4 %reduce_gradient.1 = (f32[2,16,14336]{2,1,0:T(8,128)S(1)}, f32[8,128]{1,0:T(8,128)S(1)}) custom-call(bf16[2,128,256]{2,1,0:T(8,128)(2,1)} %bitcast.13, bf16[2,128,14336]{2,1,0:T(8,128)(2,1)} %bitcast.12, s32[2,1,2]{2,1,0:T(1,128)} %cnt_hbm.1), custom_call_target="tpu_custom_call" | custom-call | tf_op jit(solution)/shard_map/reduce_gradient/pallas_call | solution.py:486
  155.1 0.0 copy-done
  155.1 0.0 copy-done.1
  155.1 1.9 %update.1 = (f32[2,16,14336]{2,1,0:T(8,128)}, f32[2,16,14336]{2,1,0:T(8,128)}) custom-call(f32[8,128]{1,0:T(8,128)S(1)} %get-tuple-element.6.stats, f32[2,16,14336]{2,1,0:T(8,128)S(1)} %get-tuple-element.7.summed, f32[2,16,14336]{2,1,0:T(8,128)S(1)} %bitcast.10, f32[2,16,14336]{2,1,0:T(8,128)S(1)} %bitcast.11), custom_call_target="tpu_custom_call" | custom-call | tf_op jit(solution)/shard_map/update/pallas_call | solution.py:525
Async XLA Ops:
  0.6 154.5 %copy-start = (f32[2,1,16,14336]{3,2,1,0:T(8,128)S(1)}, f32[2,1,16,14336]{3,2,1,0:T(8,128)}, u32[]{:S(2)}) copy-start(f32[2,1,16,14336]{3,2,1,0:T(8,128)} %param.7) | copy-start | bytes 5505028
  0.6 154.5 %copy-start.1 = (f32[2,1,16,14336]{3,2,1,0:T(8,128)S(1)}, f32[2,1,16,14336]{3,2,1,0:T(8,128)}, u32[]{:S(2)}) copy-start(f32[2,1,16,14336]{3,2,1,0:T(8,128)} %param.8) | copy-start | bytes 5505028

commit v5 on v4

--- a/solution.py
+++ b/solution.py
@@ -257,19 +257,17 @@
 
     def far_right(k):
         for b in reversed(range(2, line)):
-            pl.when(z + 1 < b)(lambda: send_right(k, own, b, None))
+            send_right(k, own, b, None)
 
     def far_left(k):
         for b in range(line - 2):
-            pl.when(z - 1 > b)(lambda: send_left(k, own, b, None))
+            send_left(k, own, b, None)
 
     def near_right(k, _):
-        for b in range(1, line):
-            pl.when(z + 1 == b)(lambda: send_right(k, own, b, None))
+        send_right(k, own, 1, None)
 
     def near_left(k, _):
-        for b in range(line - 1):
-            pl.when(z - 1 == b)(lambda: send_left(k, own, b, None))
+        send_left(k, own, line - 2, None)
 
     def both_halves(one):
         def body(k):
@@ -322,8 +320,8 @@
         when_chain(t - LAG - HOP * far, finish_early)
         when_tail(t - LAG - HOP * z, far_right)
         when_tail(t - LAG - HOP * back, far_left)
-        pl.when(t == chunks - 1 + LAG + HOP * z)(on_tail(near_right))
-        pl.when(t == chunks - 1 + LAG + HOP * back)(on_tail(near_left))
+        pl.when((t == chunks - 1 + LAG) & (z == 0))(on_tail(near_right))
+        pl.when((t == chunks - 1 + LAG) & (back == 0))(on_tail(near_left))
         pl.when(t == start_late)(send_lates)
         when_chain(t - LAG - 1, drain_y)
         when_late(t - late_behind, drain_late)

time: 157 us -> 156 us (level)
  no operation moved by 1% of the time
where the time goes in v5:
time: 156 us
  Pallas kernels  155 us (99%)
    pallas_call x1, Pallas kernels, on_device(): pl.pallas_call(functools.partial(kernel, dims), out_shape=(jax.ShapeDtype...  153 us

profile of v5, /device:TPU:0, one launch (start us, length us, event | category | flops | bytes accessed | tf_op | source)
XLA Modules:
  0.0 155.9 jit_solution(3455181457516695596)
XLA Ops:
  0.6 0.0 copy-start
  0.6 0.0 copy-start.1
  0.7 153.3 %reduce_gradient.1 = (f32[2,16,14336]{2,1,0:T(8,128)S(1)}, f32[8,128]{1,0:T(8,128)S(1)}) custom-call(bf16[2,128,256]{2,1,0:T(8,128)(2,1)} %bitcast.13, bf16[2,128,14336]{2,1,0:T(8,128)(2,1)} %bitcast.12, s32[2,1,2]{2,1,0:T(1,128)} %cnt_hbm.1), custom_call_target="tpu_custom_call" | custom-call | tf_op jit(solution)/shard_map/reduce_gradient/pallas_call | solution.py:484
  154.0 0.0 copy-done
  154.0 0.0 copy-done.1
  154.0 1.9 %update.1 = (f32[2,16,14336]{2,1,0:T(8,128)}, f32[2,16,14336]{2,1,0:T(8,128)}) custom-call(f32[8,128]{1,0:T(8,128)S(1)} %get-tuple-element.6.stats, f32[2,16,14336]{2,1,0:T(8,128)S(1)} %get-tuple-element.7.summed, f32[2,16,14336]{2,1,0:T(8,128)S(1)} %bitcast.10, f32[2,16,14336]{2,1,0:T(8,128)S(1)} %bitcast.11), custom_call_target="tpu_custom_call" | custom-call | tf_op jit(solution)/shard_map/update/pallas_call | solution.py:523
Async XLA Ops:
  0.6 153.3 %copy-start = (f32[2,1,16,14336]{3,2,1,0:T(8,128)S(1)}, f32[2,1,16,14336]{3,2,1,0:T(8,128)}, u32[]{:S(2)}) copy-start(f32[2,1,16,14336]{3,2,1,0:T(8,128)} %param.7) | copy-start | bytes 5505028
  0.6 153.3 %copy-start.1 = (f32[2,1,16,14336]{3,2,1,0:T(8,128)S(1)}, f32[2,1,16,14336]{3,2,1,0:T(8,128)}, u32[]{:S(2)}) copy-start(f32[2,1,16,14336]{3,2,1,0:T(8,128)} %param.8) | copy-start | bytes 5505028

commit v6 on v5

--- a/solution.py
+++ b/solution.py
@@ -14,7 +14,8 @@
 LAG = 6
 HOP = 3
 HOP_LATE = 3
-TAIL = 6
+TAIL = 5
+MID = 4
 SPLIT = 4
 AHEAD = 6
 RING = 8
@@ -36,6 +37,7 @@
     half = line * rows
     chunks = layers * per_layer
     first_tail = chunks - TAIL
+    first_mid = chunks - (MID if line > 3 else 0)
     z, e, s = lax.axis_index("dp"), lax.axis_index("expert"), lax.axis_index("shard")
     y, c = s // CORES, s % CORES
     me = z * shards + s
@@ -255,13 +257,22 @@
         for b in range(line - 1):
             send_left(k, base, b, late)
 
+    def sooner(k, b, last):
+        return k < first_mid if b == last and line > 3 else k >= 0
+
     def far_right(k):
         for b in reversed(range(2, line)):
-            send_right(k, own, b, None)
+            pl.when(sooner(k, b, 2))(lambda: send_right(k, own, b, None))
 
     def far_left(k):
         for b in range(line - 2):
-            send_left(k, own, b, None)
+            pl.when(sooner(k, b, line - 3))(lambda: send_left(k, own, b, None))
+
+    def mid_right(k, _):
+        send_right(k, own, 2, None)
+
+    def mid_left(k, _):
+        send_left(k, own, line - 3, None)
 
     def near_right(k, _):
         send_right(k, own, 1, None)
@@ -304,6 +315,9 @@
 
     def on_tail(body):
         return lambda: lax.fori_loop(first_tail, chunks, body, None)
+
+    def on_mid(body):
+        return lambda: lax.fori_loop(first_mid, chunks, body, None)
 
     def step(t, _):
         pl.when(t + AHEAD < chunks)(lambda: fetch(t + AHEAD).start())
@@ -320,6 +334,8 @@
         when_chain(t - LAG - HOP * far, finish_early)
         when_tail(t - LAG - HOP * z, far_right)
         when_tail(t - LAG - HOP * back, far_left)
+        pl.when(t == chunks - 1 + LAG + HOP * z)(on_mid(mid_right))
+        pl.when(t == chunks - 1 + LAG + HOP * back)(on_mid(mid_left))
         pl.when((t == chunks - 1 + LAG) & (z == 0))(on_tail(near_right))
         pl.when((t == chunks - 1 + LAG) & (back == 0))(on_tail(near_left))
         pl.when(t == start_late)(send_lates)

time: 156 us -> 156 us (level)
  no operation moved by 1% of the time
where the time goes in v6:
time: 156 us
  Pallas kernels  155 us (99%)
    pallas_call x1, Pallas kernels, on_device(): pl.pallas_call(functools.partial(kernel, dims), out_shape=(jax.ShapeDtype...  153 us

profile of v6, /device:TPU:0, one launch (start us, length us, event | category | flops | bytes accessed | tf_op | source)
XLA Modules:
  0.0 155.6 jit_solution(15219039619469821374)
XLA Ops:
  0.6 0.0 copy-start
  0.6 0.0 copy-start.1
  0.7 153.0 %reduce_gradient.1 = (f32[2,16,14336]{2,1,0:T(8,128)S(1)}, f32[8,128]{1,0:T(8,128)S(1)}) custom-call(bf16[2,128,256]{2,1,0:T(8,128)(2,1)} %bitcast.13, bf16[2,128,14336]{2,1,0:T(8,128)(2,1)} %bitcast.12, s32[2,1,2]{2,1,0:T(1,128)} %cnt_hbm.1), custom_call_target="tpu_custom_call" | custom-call | tf_op jit(solution)/shard_map/reduce_gradient/pallas_call | solution.py:500
  153.6 0.0 copy-done
  153.6 0.0 copy-done.1
  153.6 1.9 %update.1 = (f32[2,16,14336]{2,1,0:T(8,128)}, f32[2,16,14336]{2,1,0:T(8,128)}) custom-call(f32[8,128]{1,0:T(8,128)S(1)} %get-tuple-element.6.stats, f32[2,16,14336]{2,1,0:T(8,128)S(1)} %get-tuple-element.7.summed, f32[2,16,14336]{2,1,0:T(8,128)S(1)} %bitcast.10, f32[2,16,14336]{2,1,0:T(8,128)S(1)} %bitcast.11), custom_call_target="tpu_custom_call" | custom-call | tf_op jit(solution)/shard_map/update/pallas_call | solution.py:539
Async XLA Ops:
  0.6 153.0 %copy-start = (f32[2,1,16,14336]{3,2,1,0:T(8,128)S(1)}, f32[2,1,16,14336]{3,2,1,0:T(8,128)}, u32[]{:S(2)}) copy-start(f32[2,1,16,14336]{3,2,1,0:T(8,128)} %param.7) | copy-start | bytes 5505028
  0.6 153.0 %copy-start.1 = (f32[2,1,16,14336]{3,2,1,0:T(8,128)S(1)}, f32[2,1,16,14336]{3,2,1,0:T(8,128)}, u32[]{:S(2)}) copy-start(f32[2,1,16,14336]{3,2,1,0:T(8,128)} %param.8) | copy-start | bytes 5505028

commit v7 on v6

--- a/solution.py
+++ b/solution.py
@@ -15,7 +15,7 @@
 HOP = 3
 HOP_LATE = 3
 TAIL = 5
-MID = 4
+MID = 3
 SPLIT = 4
 AHEAD = 6
 RING = 8

time: 156 us -> 156 us (level)
  no operation moved by 1% of the time
where the time goes in v7:
time: 156 us; the launch traced here: 155 us
  Pallas kernels  155 us (99%)
    pallas_call x1, Pallas kernels, on_device(): pl.pallas_call(functools.partial(kernel, dims), out_shape=(jax.ShapeDtype...  153 us

profile of v7, /device:TPU:0, one launch (start us, length us, event | category | flops | bytes accessed | tf_op | source)
XLA Modules:
  0.0 155.4 jit_solution(13640080810339746780)
XLA Ops:
  0.6 0.0 copy-start
  0.6 0.0 copy-start.1
  0.7 152.7 %reduce_gradient.1 = (f32[2,16,14336]{2,1,0:T(8,128)S(1)}, f32[8,128]{1,0:T(8,128)S(1)}) custom-call(bf16[2,128,256]{2,1,0:T(8,128)(2,1)} %bitcast.13, bf16[2,128,14336]{2,1,0:T(8,128)(2,1)} %bitcast.12, s32[2,1,2]{2,1,0:T(1,128)} %cnt_hbm.1), custom_call_target="tpu_custom_call" | custom-call | tf_op jit(solution)/shard_map/reduce_gradient/pallas_call | solution.py:500
  153.4 0.0 copy-done
  153.4 0.0 copy-done.1
  153.4 1.9 %update.1 = (f32[2,16,14336]{2,1,0:T(8,128)}, f32[2,16,14336]{2,1,0:T(8,128)}) custom-call(f32[8,128]{1,0:T(8,128)S(1)} %get-tuple-element.6.stats, f32[2,16,14336]{2,1,0:T(8,128)S(1)} %get-tuple-element.7.summed, f32[2,16,14336]{2,1,0:T(8,128)S(1)} %bitcast.10, f32[2,16,14336]{2,1,0:T(8,128)S(1)} %bitcast.11), custom_call_target="tpu_custom_call" | custom-call | tf_op jit(solution)/shard_map/update/pallas_call | solution.py:539
Async XLA Ops:
  0.6 152.8 %copy-start = (f32[2,1,16,14336]{3,2,1,0:T(8,128)S(1)}, f32[2,1,16,14336]{3,2,1,0:T(8,128)}, u32[]{:S(2)}) copy-start(f32[2,1,16,14336]{3,2,1,0:T(8,128)} %param.7) | copy-start | bytes 5505028
  0.6 152.8 %copy-start.1 = (f32[2,1,16,14336]{3,2,1,0:T(8,128)S(1)}, f32[2,1,16,14336]{3,2,1,0:T(8,128)}, u32[]{:S(2)}) copy-start(f32[2,1,16,14336]{3,2,1,0:T(8,128)} %param.8) | copy-start | bytes 5505028
